TPU v7x, 32 devices: a whole 2x2x4 slice. The times are simulated.
32 devices in a mesh: row: 16 (over z, x, core), col: 2 (over y).
Axes of the slice: x: 2, y: 2, z: 4, core: 2. Of those that a mesh axis runs over, the one named last changes fastest.
Arguments:
- occupied_waves: bfloat16 [1024, 32768], P('row', 'col'), may hold values from -6 to 6
- virtual_waves: bfloat16 [512, 32768], P('row', 'col'), may hold values from -6 to 6
- occupied_decay: float32 [1024], replicated, may hold values from 0.02 to 1
- virtual_decay: float32 [512], replicated, may hold values from 0.02 to 1
Outputs:
- spectrum_real: float32 [512, 32, 1024], P('row', 'col')
- spectrum_imaginary: float32 [512, 32, 1024], P('row', 'col')
All inputs are finite; a program needn't handle non-finite values.
Results may differ from a plain program's by a relative error of at most 0.0041.
Values may be sent and summed in bfloat16 or wider, within the bound.
A program may use at most 128 MiB of HBM per device.

v0:
```python
import math
import jax
import jax.numpy as jnp
from jax import lax
from jax.sharding import PartitionSpec as P

NOCC = 1024
NVIR = 512
NA = 32
NB = 32
NC = 32
ROWS_DEV = 32
NGRID = 32768


def tables(length):
    index = jnp.arange(length, dtype=jnp.int32)
    phase = index[:, None] * index[None, :] % length
    angle = phase.astype(jnp.float32) * (2.0 * math.pi / length)
    return (jnp.cos(angle), jnp.sin(angle))


def apply_table(form, data, table):
    return jnp.einsum(form, data, table, precision=lax.Precision.HIGHEST)


def real_step(data, form, length):
    cosine, sine = tables(length)
    return (apply_table(form, data, cosine), -apply_table(form, data, sine))


def complex_step(real_part, imag_part, form, length):
    cosine, sine = tables(length)
    new_real = apply_table(form, real_part, cosine) + apply_table(form, imag_part, sine)
    new_imag = apply_table(form, imag_part, cosine) - apply_table(form, real_part, sine)
    return (new_real, new_imag)


def scale_rows(waves, decay):
    return (waves * decay[:, None]).astype(jnp.bfloat16)


def place(waves, window, start_col):
    block_cols = waves.shape[1]
    buffer = jnp.zeros((waves.shape[0], window + block_cols), jnp.bfloat16)
    buffer = lax.dynamic_update_slice(buffer, waves, (jnp.int32(0), start_col))
    return buffer[:, :window]


def on_device(occupied_waves, virtual_waves, occupied_decay, virtual_decay):
    block_cols = occupied_waves.shape[1]
    row_count = lax.axis_size("row")
    contract = (((0,), (0,)), ((), ()))
    factor = -1.0 / math.sqrt(NOCC * NVIR)
    window = ROWS_DEV * row_count
    start_col = lax.axis_index("col") * block_cols
    plane_cols = NB * NC
    per_col = block_cols // plane_cols
    spread = row_count // per_col
    sub_rows = ROWS_DEV // spread

    def spread_planes(waves):
        share = waves.shape[0]
        shaped = waves.reshape(share, per_col, 1, plane_cols)
        shaped = jnp.broadcast_to(shaped, (share, per_col, spread, plane_cols))
        return shaped.reshape(share, row_count * plane_cols)

    def pick_rows(waves):
        share = waves.shape[0]
        shaped = place(waves, window, start_col).reshape(share, row_count, spread, sub_rows)
        shaped = jnp.transpose(shaped, (0, 2, 1, 3))[:, None]
        shaped = jnp.broadcast_to(shaped, (share, per_col, spread, row_count, sub_rows))
        return shaped.reshape(share, row_count * row_count * sub_rows)

    plane_occ, plane_vir = (
        lax.all_to_all(
            spread_planes(occupied_waves), "row", split_axis=1, concat_axis=0, tiled=True
        ),
        lax.all_to_all(
            spread_planes(virtual_waves), "row", split_axis=1, concat_axis=0, tiled=True
        ),
    )
    part_occ, part_vir = (
        lax.all_to_all(pick_rows(occupied_waves), "row", split_axis=1, concat_axis=0, tiled=True),
        lax.all_to_all(pick_rows(virtual_waves), "row", split_axis=1, concat_axis=0, tiled=True),
    )
    occ_rows, vir_rows = (
        lax.psum(part_occ.astype(jnp.float32).astype(jnp.bfloat16), "col").astype(jnp.float32),
        lax.psum(part_vir.astype(jnp.float32).astype(jnp.bfloat16), "col").astype(jnp.float32),
    )
    occ_rows = scale_rows(occ_rows, occupied_decay)
    vir_rows = scale_rows(vir_rows, virtual_decay)
    green_occ = lax.dot_general(plane_occ, occ_rows, contract, preferred_element_type=jnp.float32)
    green_vir = lax.dot_general(plane_vir, vir_rows, contract, preferred_element_type=jnp.float32)
    polar = green_occ * green_vir * factor
    cube = polar.reshape(1, NB, NC, row_count * sub_rows)
    real_part, imag_part = real_step(cube, "abcr,cw->wabr", NC)
    real_part, imag_part = complex_step(real_part, imag_part, "wabr,bv->wavr", NB)
    blocked = (NC, 1, NB, row_count, sub_rows)
    real_part, imag_part = (
        lax.all_to_all(
            lax.all_to_all(
                real_part.reshape(blocked), "row", split_axis=3, concat_axis=3, tiled=True
            ),
            "col",
            split_axis=0,
            concat_axis=1,
            tiled=True,
        ),
        lax.all_to_all(
            lax.all_to_all(
                imag_part.reshape(blocked), "row", split_axis=3, concat_axis=3, tiled=True
            ),
            "col",
            split_axis=0,
            concat_axis=1,
            tiled=True,
        ),
    )

    def settle(part):
        kc_share = part.shape[0]
        part = part.reshape(kc_share, part.shape[1], NB, per_col, spread, sub_rows)
        part = jnp.transpose(part, (0, 1, 3, 2, 4, 5))
        return part.reshape(kc_share, NA, NB, ROWS_DEV)

    real_part, imag_part = complex_step(settle(real_part), settle(imag_part), "wavr,au->rwuv", NA)
    normal = 1.0 / math.sqrt(NGRID)
    final_shape = (real_part.shape[0], real_part.shape[1], NA * NB)
    return ((real_part * normal).reshape(final_shape), (imag_part * normal).reshape(final_shape))


def solution(mesh):
    in_specs = (P("row", "col"), P("row", "col"), P(), P())
    out_specs = (P("row", "col", None), P("row", "col", None))
    return jax.shard_map(
        on_device, mesh=mesh, in_specs=in_specs, out_specs=out_specs, check_vma=False
    )
```

profile of v0, /device:TPU:10, one launch (start us, length us, event | category | flops | bytes accessed | tf_op | source)
XLA Modules:
  0.0 507.3 jit_solution(10017124884010591523)
XLA Ops:
  9.4 6.2 %all-to-all-start.2 = ((bf16[32,16,512]{2,0,1:T(8,128)(2,1)}), bf16[32,16,512]{2,0,1:T(8,128)(2,1)S(1)}, u32[]{:S(2)}, u32[]{:S(2)}) async-start(bf16[32,16,512]{2,0,1:T(8,128)(2,1)} %broadcast_in_dim.11), calls=%async_computation.2 | async-start | bytes 1048576 | tf_op jit(solution)/shard_map/all_to_all | solution.py:85
  16.1 12.9 %all-to-all-done.2 = bf16[32,16,512]{2,0,1:T(8,128)(2,1)S(1)} async-done(((bf16[32,16,512]{2,0,1:T(8,128)(2,1)}), bf16[32,16,512]{2,0,1:T(8,128)(2,1)S(1)}, u32[]{:S(2)}, u32[]{:S(2)}) %all-to-all-start.2) | async-done | bytes 524320 | tf_op jit(solution)/shard_map/all_to_all | solution.py:85
  30.1 5.2 %all-to-all-start = ((bf16[64,16,512]{2,0,1:T(8,128)(2,1)}), bf16[64,16,512]{2,0,1:T(8,128)(2,1)S(1)}, u32[]{:S(2)}, u32[]{:S(2)}) async-start(bf16[64,16,512]{2,0,1:T(8,128)(2,1)} %broadcast_in_dim.9), calls=%async_computation | async-start | bytes 2097152 | tf_op jit(solution)/shard_map/all_to_all | solution.py:84
  36.8 23.0 %all-to-all-done = bf16[64,16,512]{2,0,1:T(8,128)(2,1)S(1)} async-done(((bf16[64,16,512]{2,0,1:T(8,128)(2,1)}), bf16[64,16,512]{2,0,1:T(8,128)(2,1)S(1)}, u32[]{:S(2)}, u32[]{:S(2)}) %all-to-all-start) | async-done | bytes 1048608 | tf_op jit(solution)/shard_map/all_to_all | solution.py:84
  60.8 5.2 %all-to-all-start.1 = ((bf16[64,16,1024]{2,0,1:T(8,128)(2,1)}), bf16[64,16,1024]{2,0,1:T(8,128)(2,1)S(1)}, u32[]{:S(2)}, u32[]{:S(2)}) async-start(bf16[64,16,1024]{2,0,1:T(8,128)(2,1)} %bitcast.123), calls=%async_computation.1 | async-start | bytes 4194304 | tf_op jit(solution)/shard_map/all_to_all | solution.py:76
  67.1 46.1 %all-to-all-done.1 = bf16[64,16,1024]{2,0,1:T(8,128)(2,1)S(1)} async-done(((bf16[64,16,1024]{2,0,1:T(8,128)(2,1)}), bf16[64,16,1024]{2,0,1:T(8,128)(2,1)S(1)}, u32[]{:S(2)}, u32[]{:S(2)}) %all-to-all-start.1) | async-done | bytes 2097184 | tf_op jit(solution)/shard_map/all_to_all | solution.py:76
  113.2 5.1 all-to-all-start.3
  119.0 55.5 %all-reduce.3.cloned.1.call-done = (bf16[1024,512]{1,0:T(8,128)(2,1)}, bf16[512,512]{1,0:T(8,128)(2,1)}) async-done(((bf16[1024,512]{1,0:T(8,128)(2,1)}, bf16[512,512]{1,0:T(8,128)(2,1)}), (bf16[1024,512]{1,0:T(8,128)(2,1)}, bf16[512,512]{1,0:T(8,128)(2,1)})) %all-reduce.3.cloned.1.call-update) | async-done | bytes 1572880 | tf_op jit(solution)/shard_map/psum | solution.py:88
  174.5 3.9 fusion.12
  178.5 3.9 multiply_bitcast_fusion.2
  187.7 4.3 fusion.29
  195.0 4.4 subtract_bitcast_fusion
  199.4 6.4 %reshape.86 = f32[32,1,32,16,32]{4,3,2,0,1:T(8,128)} reshape(f32[32,1,32,512]{3,2,0,1:T(8,128)} %subtract_bitcast_fusion) | data formatting | bytes 4194304 | tf_op jit(solution)/shard_map/reshape | solution.py:112
  205.8 9.3 %copy.71 = f32[32,1,32,16,32]{4,2,0,1,3:T(8,128)} copy(f32[32,1,32,16,32]{4,3,2,0,1:T(8,128)} %reshape.86) | data formatting | bytes 4194304 | tf_op jit(solution)/shard_map/reshape | solution.py:112
  215.1 8.6 %reshape.99 = f32[16,1,32768]{2,1,0:T(1,128)} reshape(f32[16,1,32,32,32]{4,3,2,1,0:T(8,128)} %bitcast.113) | data formatting | bytes 4194304
  223.7 6.1 %all-to-all-start.6 = ((f32[16,1,32768]{2,1,0:T(1,128)}), f32[16,1,32768]{2,1,0:T(1,128)}, u32[]{:S(2)}, u32[]{:S(2)}) async-start(f32[16,1,32768]{2,1,0:T(1,128)} %reshape.99), calls=%async_computation.6 | async-start | bytes 4194304 | tf_op jit(solution)/shard_map/all_to_all | solution.py:111
  229.7 4.6 fusion.2
  234.3 4.4 add_bitcast_fusion
  238.7 6.2 %reshape.83 = f32[32,1,32,16,32]{4,3,2,0,1:T(8,128)} reshape(f32[32,1,32,512]{3,2,0,1:T(8,128)} %add_bitcast_fusion) | data formatting | bytes 4194304 | tf_op jit(solution)/shard_map/reshape | solution.py:103
  244.9 9.3 %copy.72 = f32[32,1,32,16,32]{4,2,0,1,3:T(8,128)} copy(f32[32,1,32,16,32]{4,3,2,0,1:T(8,128)} %reshape.83) | data formatting | bytes 4194304 | tf_op jit(solution)/shard_map/reshape | solution.py:103
  254.2 8.6 %reshape.95 = f32[16,1,32768]{2,1,0:T(1,128)} reshape(f32[16,1,32,32,32]{4,3,2,1,0:T(8,128)} %bitcast.114) | data formatting | bytes 4194304
  262.7 14.2 %all-to-all-done.6 = f32[16,1,32768]{2,1,0:T(1,128)} async-done(((f32[16,1,32768]{2,1,0:T(1,128)}), f32[16,1,32768]{2,1,0:T(1,128)}, u32[]{:S(2)}, u32[]{:S(2)}) %all-to-all-start.6) | async-done | bytes 2097184 | tf_op jit(solution)/shard_map/all_to_all | solution.py:111
  277.0 5.6 %all-to-all-start.4 = ((f32[16,1,32768]{2,1,0:T(1,128)}), f32[16,1,32768]{2,1,0:T(1,128)}, u32[]{:S(2)}, u32[]{:S(2)}) async-start(f32[16,1,32768]{2,1,0:T(1,128)} %reshape.95), calls=%async_computation.4 | async-start | bytes 4194304 | tf_op jit(solution)/shard_map/all_to_all | solution.py:102
  283.2 7.3 %reduce.2 = f32[16,32768]{1,0:T(8,128)S(1)} reduce(f32[16,1,32768]{2,1,0:T(1,128)} %all-to-all-done.6, f32[]{:T(128)} %broadcast.102), dimensions={1}, to_apply=%all_to_all.98.reduce_sub_computation | reduce | bytes 4194308 | tf_op jit(solution)/shard_map/all_to_all | solution.py:111
  290.4 4.9 reshape.100
  295.4 14.2 %copy.45 = f32[32,1,32,16,32]{4,3,2,1,0:T(8,128)} copy(f32[32,1,32,16,32]{4,2,0,1,3:T(8,128)} %bitcast.115) | data formatting | bytes 4194304 | tf_op jit(solution)/shard_map/all_to_all | solution.py:111
  309.5 6.8 %reshape.101 = f32[2,1,262144]{2,1,0:T(1,128)} reshape(f32[32,1,32,16,32]{4,3,2,1,0:T(8,128)} %copy.45) | data formatting | bytes 4194304
  316.4 13.3 %all-to-all-done.4 = f32[16,1,32768]{2,1,0:T(1,128)} async-done(((f32[16,1,32768]{2,1,0:T(1,128)}), f32[16,1,32768]{2,1,0:T(1,128)}, u32[]{:S(2)}, u32[]{:S(2)}) %all-to-all-start.4) | async-done | bytes 2097184 | tf_op jit(solution)/shard_map/all_to_all | solution.py:102
  329.7 5.0 all-to-all-start.7
  334.7 7.3 %reduce = f32[16,32768]{1,0:T(8,128)S(1)} reduce(f32[16,1,32768]{2,1,0:T(1,128)} %all-to-all-done.4, f32[]{:T(128)} %broadcast.102), dimensions={1}, to_apply=%all_to_all.94.reduce_sub_computation | reduce | bytes 4194308 | tf_op jit(solution)/shard_map/all_to_all | solution.py:102
  342.0 4.8 reshape.96
  346.7 14.2 %copy.40 = f32[32,1,32,16,32]{4,3,2,1,0:T(8,128)} copy(f32[32,1,32,16,32]{4,2,0,1,3:T(8,128)} %bitcast.116) | data formatting | bytes 4194304 | tf_op jit(solution)/shard_map/all_to_all | solution.py:102
  360.9 6.8 %reshape.97 = f32[2,1,262144]{2,1,0:T(1,128)} reshape(f32[32,1,32,16,32]{4,3,2,1,0:T(8,128)} %copy.40) | data formatting | bytes 4194304
  367.8 4.8 all-to-all-start.5
  372.6 8.5 %reduce.3 = f32[2,262144]{1,0:T(2,128)S(1)} reduce(f32[2,1,262144]{2,1,0:T(1,128)} %all-to-all-done.7, f32[]{:T(128)} %broadcast.102), dimensions={1}, to_apply=%all_to_all.99.reduce_sub_computation | reduce | bytes 4194308 | tf_op jit(solution)/shard_map/all_to_all | solution.py:110
  381.1 6.4 %reshape.102 = f32[32,1,32,16,32]{4,3,2,1,0:T(8,128)} reshape(f32[2,262144]{1,0:T(2,128)S(1)} %reduce.3) | data formatting | bytes 4194304
  387.5 7.7 %copy.46 = f32[2,16,1,32,16,32]{5,4,0,3,1,2:T(8,128)} copy(f32[2,16,1,32,16,32]{5,4,3,1,0,2:T(8,128)} %bitcast.117) | data formatting | bytes 4194304 | tf_op jit(solution)/shard_map/all_to_all | solution.py:110
  398.3 8.2 %reduce.1 = f32[2,262144]{1,0:T(2,128)S(1)} reduce(f32[2,1,262144]{2,1,0:T(1,128)} %all-to-all-done.5, f32[]{:T(128)} %broadcast.102), dimensions={1}, to_apply=%all_to_all.95.reduce_sub_computation | reduce | bytes 4194308 | tf_op jit(solution)/shard_map/all_to_all | solution.py:101
  406.6 6.4 %reshape.98 = f32[32,1,32,16,32]{4,3,2,1,0:T(8,128)} reshape(f32[2,262144]{1,0:T(2,128)S(1)} %reduce.1) | data formatting | bytes 4194304
  413.0 4.6 copy.41
  417.6 9.5 %fusion.22 = f32[32,16,32,32]{3,0,2,1:T(8,128)} fusion(f32[16,32,32,32]{3,1,2,0:T(8,128)S(1)} %bitcast.111), kind=kOutput, calls=%fused_computation.31 | convolution fusion | flops 201340928 | bytes 4194304 | tf_op jit(solution)/shard_map/wavr,au->rwuv/dot_general | solution.py:24
  427.1 9.8 %fusion.20 = f32[32,16,32,32]{3,0,2,1:T(8,128)} fusion(f32[16,32,32,32]{3,1,2,0:T(8,128)S(1)} %bitcast.109), kind=kOutput, calls=%fused_computation.29 | convolution fusion | flops 201340928 | bytes 4194304 | tf_op jit(solution)/shard_map/wavr,au->rwuv/dot_general | solution.py:24
  436.9 12.1 %multiply_bitcast_fusion.1 = f32[32,16,32,32]{0,2,3,1:T(8,128)} fusion(f32[32,16,32,32]{3,0,2,1:T(8,128)} %fusion.22, f32[16,32,32,32]{3,1,2,0:T(8,128)S(1)} %bitcast.110), kind=kOutput, calls=%fused_computation.1 | convolution fusion | flops 202389504 | bytes 6291456 | tf_op jit(solution)/shard_map/wavr,au->rwuv/dot_general | solution.py:24
  449.0 12.4 %multiply_bitcast_fusion = f32[32,16,32,32]{0,2,3,1:T(8,128)} fusion(f32[32,16,32,32]{3,0,2,1:T(8,128)} %fusion.20, f32[16,32,32,32]{3,1,2,0:T(8,128)S(1)} %bitcast.112), kind=kOutput, calls=%fused_computation | convolution fusion | flops 202389504 | bytes 6291456 | tf_op jit(solution)/shard_map/wavr,au->rwuv/dot_general | solution.py:24
  461.4 11.7 %copy.48 = f32[32,16,32,32]{3,2,1,0:T(8,128)} copy(f32[32,16,32,32]{0,2,3,1:T(8,128)} %multiply_bitcast_fusion) | data formatting | bytes 4194304 | tf_op jit(solution)/shard_map/mul | solution.py:130
  473.1 7.7 %reshape.90 = f32[32,16,1024]{2,1,0:T(8,128)} reshape(f32[32,16,32,32]{3,2,1,0:T(8,128)} %copy.48) | data formatting | bytes 4194304 | tf_op jit(solution)/shard_map/reshape | solution.py:130
  480.8 11.7 %copy.47 = f32[32,16,32,32]{3,2,1,0:T(8,128)} copy(f32[32,16,32,32]{0,2,3,1:T(8,128)} %multiply_bitcast_fusion.1) | data formatting | bytes 4194304 | tf_op jit(solution)/shard_map/mul | solution.py:130
  492.5 7.7 %reshape.89 = f32[32,16,1024]{2,1,0:T(8,128)} reshape(f32[32,16,32,32]{3,2,1,0:T(8,128)} %copy.47) | data formatting | bytes 4194304 | tf_op jit(solution)/shard_map/reshape | solution.py:130
  (40 shorter events, 20.1 us)
Async XLA Ops:
  8.6 7.3 %copy-start.2 = (bf16[64,16384]{1,0:T(8,128)(2,1)S(1)}, bf16[64,16384]{1,0:T(8,128)(2,1)}, u32[]{:S(2)}) copy-start(bf16[64,16384]{1,0:T(8,128)(2,1)} %param.4) | copy-start | bytes 6291460
  9.4 19.5 %all-to-all-start.2 = ((bf16[32,16,512]{2,0,1:T(8,128)(2,1)}), bf16[32,16,512]{2,0,1:T(8,128)(2,1)S(1)}, u32[]{:S(2)}, u32[]{:S(2)}) async-start(bf16[32,16,512]{2,0,1:T(8,128)(2,1)} %broadcast_in_dim.11), calls=%async_computation.2 | async-start | bytes 1048576 | tf_op jit(solution)/shard_map/all_to_all | solution.py:85
  29.0 1.1 copy-start.5
  30.1 29.7 %all-to-all-start = ((bf16[64,16,512]{2,0,1:T(8,128)(2,1)}), bf16[64,16,512]{2,0,1:T(8,128)(2,1)S(1)}, u32[]{:S(2)}, u32[]{:S(2)}) async-start(bf16[64,16,512]{2,0,1:T(8,128)(2,1)} %broadcast_in_dim.9), calls=%async_computation | async-start | bytes 2097152 | tf_op jit(solution)/shard_map/all_to_all | solution.py:84
  59.9 1.0 copy-start.4
  60.8 5.2 %copy-start.3 = (bf16[32,16384]{1,0:T(8,128)(2,1)S(1)}, bf16[32,16384]{1,0:T(8,128)(2,1)}, u32[]{:S(2)}) copy-start(bf16[32,16384]{1,0:T(8,128)(2,1)} %param.5) | copy-start | bytes 3145732
  60.8 52.4 %all-to-all-start.1 = ((bf16[64,16,1024]{2,0,1:T(8,128)(2,1)}), bf16[64,16,1024]{2,0,1:T(8,128)(2,1)S(1)}, u32[]{:S(2)}, u32[]{:S(2)}) async-start(bf16[64,16,1024]{2,0,1:T(8,128)(2,1)} %bitcast.123), calls=%async_computation.1 | async-start | bytes 4194304 | tf_op jit(solution)/shard_map/all_to_all | solution.py:76
  67.1 107.4 %copy-start.6 = (f32[1024]{0:T(1024)S(1)}, f32[1024]{0:T(1024)}, u32[]{:S(2)}) copy-start(f32[1024]{0:T(1024)} %param.6) | copy-start | bytes 12292
  113.2 65.3 %all-to-all-start.3 = ((bf16[32,16,1024]{2,0,1:T(8,128)(2,1)}), bf16[32,16,1024]{2,0,1:T(8,128)(2,1)S(1)}, u32[]{:S(2)}, u32[]{:S(2)}) async-start(bf16[32,16,1024]{2,0,1:T(8,128)(2,1)} %bitcast.126), calls=%async_computation.3 | async-start | bytes 2097152 | tf_op jit(solution)/shard_map/all_to_all | solution.py:79
  118.3 56.3 %all-reduce.3.cloned.1.call-start = ((), (), s32[]{:S(2)}) async-start(), calls=%async_computation.8 | async-start | bytes 3145728 | tf_op jit(solution)/shard_map/psum | solution.py:88
  174.5 3.9 copy-start.7
  184.5 1.3 copy-start.1
  187.7 4.3 copy-start
  223.7 53.3 %all-to-all-start.6 = ((f32[16,1,32768]{2,1,0:T(1,128)}), f32[16,1,32768]{2,1,0:T(1,128)}, u32[]{:S(2)}, u32[]{:S(2)}) async-start(f32[16,1,32768]{2,1,0:T(1,128)} %reshape.99), calls=%async_computation.6 | async-start | bytes 4194304 | tf_op jit(solution)/shard_map/all_to_all | solution.py:111
  277.0 52.7 %all-to-all-start.4 = ((f32[16,1,32768]{2,1,0:T(1,128)}), f32[16,1,32768]{2,1,0:T(1,128)}, u32[]{:S(2)}, u32[]{:S(2)}) async-start(f32[16,1,32768]{2,1,0:T(1,128)} %reshape.95), calls=%async_computation.4 | async-start | bytes 4194304 | tf_op jit(solution)/shard_map/all_to_all | solution.py:102
  329.7 38.1 %all-to-all-start.7 = ((f32[2,1,262144]{2,1,0:T(1,128)}), f32[2,1,262144]{2,1,0:T(1,128)}, u32[]{:S(2)}, u32[]{:S(2)}) async-start(f32[2,1,262144]{2,1,0:T(1,128)} %reshape.101), calls=%async_computation.7 | async-start | bytes 4194304 | tf_op jit(solution)/shard_map/all_to_all | solution.py:110
  367.8 30.6 %all-to-all-start.5 = ((f32[2,1,262144]{2,1,0:T(1,128)}), f32[2,1,262144]{2,1,0:T(1,128)}, u32[]{:S(2)}, u32[]{:S(2)}) async-start(f32[2,1,262144]{2,1,0:T(1,128)} %reshape.97), calls=%async_computation.5 | async-start | bytes 4194304 | tf_op jit(solution)/shard_map/all_to_all | solution.py:101
  413.0 14.1 %slice-start = ((s8[8388608]{0:T(1024)(128)(4,1)}), s8[4194304]{0:T(1024)(128)(4,1)S(1)}, s32[]{:S(2)}) async-start(s8[8388608]{0:T(1024)(128)(4,1)} %bitcast.107), calls=%async_computation.9 | async-start | bytes 8388608
  417.6 9.5 %slice-start.1 = ((s8[8388608]{0:T(1024)(128)(4,1)}), s8[4194304]{0:T(1024)(128)(4,1)S(1)}, s32[]{:S(2)}) async-start(s8[8388608]{0:T(1024)(128)(4,1)} %bitcast.107), calls=%async_computation.10 | async-start | bytes 8388608
Sparse Core Ops, SparseCore 0:
  122.0 52.4 all-reduce.2
where the time goes:
time: 513 us; the launch traced here: 507 us
  local copies, waits for them, and re-layouts  175 us (34%)
  waiting for transfers between devices  169 us (33%)
  matrix products  74.2 us (14%)
  starting transfers between devices  43.2 us (8%)
  other arithmetic  31.2 us (6%)
  between operations  14.5 us (3%)
    dot_general x10, matrix products, apply_table(): return jnp.einsum(form, data, table, precision=lax.Precision.HIGHEST)  66.3 us
    unnamed x28, local copies, waits for them, and re-layouts  55.6 us
    psum x1, waiting for transfers between devices, on_device(): lax.psum(part_occ.astype(jnp.float32).astype(jnp.bfloat16), 'col')  55.5 us
    all_to_all x1, waiting for transfers between devices, on_device(): lax.all_to_all(spread_planes(occupied_waves), 'row', split_axis=1, concat...  46.1 us
    all_to_all x1, waiting for transfers between devices, on_device(): lax.all_to_all(pick_rows(occupied_waves), 'row', split_axis=1, concat_axi...  23 us
    reshape x2, local copies, waits for them, and re-layouts, on_device(): imag_part.reshape(blocked)  15.7 us
    reshape x2, local copies, waits for them, and re-layouts, on_device(): real_part.reshape(blocked)  15.5 us
    all_to_all x2, local copies, waits for them, and re-layouts, on_device(): lax.all_to_all(real_part.reshape(blocked), 'row', split_axis=3, concat_ax...  14.8 us
  transfers between devices with their start and end apart: 9, of which 7 were waited for; matrix products, arithmetic and copies ran while one was open for 26% of the time, Pallas kernels for 0%

commit v1 on v0

--- a/solution.py
+++ b/solution.py
@@ -11,6 +11,32 @@
 NC = 32
 ROWS_DEV = 32
 NGRID = 32768
+
+
+def slots_settle(array_here, k_dim, slab_in):
+    formed, reached = (array_here.shape[:k_dim], array_here.shape[k_dim + 1 :])
+    return jnp.moveaxis(array_here.reshape(*formed, slab_in, -1, *reached), k_dim, 0)
+
+
+def _attach_sheets(state, dim_i):
+    piece_next = list(state.shape[1:])
+    piece_next[dim_i] *= state.shape[0]
+    return jnp.moveaxis(state, 0, dim_i).reshape(piece_next)
+
+
+def _render_desk(shard_in, mesh_dim, block_here, my_tile):
+    n_now, val2 = (lax.axis_size(mesh_dim), lax.axis_index(mesh_dim))
+    view_out = slots_settle(shard_in, block_here, n_now)
+    entries = [view_out[val2]]
+    pp = 1
+    while pp < n_now:
+        base_arr = view_out[val2 ^ pp]
+        entries.append(
+            lax.ppermute(base_arr, mesh_dim, [(tick, tick ^ pp) for tick in range(n_now)])
+        )
+        pp = pp + 1
+    view_out = jnp.stack(entries)[val2 ^ jnp.arange(n_now)]
+    return _attach_sheets(view_out, my_tile)
 
 
 def tables(length):
@@ -73,9 +99,7 @@
         return shaped.reshape(share, row_count * row_count * sub_rows)
 
     plane_occ, plane_vir = (
-        lax.all_to_all(
-            spread_planes(occupied_waves), "row", split_axis=1, concat_axis=0, tiled=True
-        ),
+        _render_desk(spread_planes(occupied_waves), "row", 1, 0),
         lax.all_to_all(
             spread_planes(virtual_waves), "row", split_axis=1, concat_axis=0, tiled=True
         ),

time: 513 us -> 468 us (0.912)
  waiting for transfers between devices: 169 us -> 95.3 us
  local copies, waits for them, and re-layouts: 175 us -> 196 us
  starting transfers between devices: 43.2 us -> 55.3 us
  matrix products: 74.2 us -> 67.9 us
    ppermute x0 -> x15, waiting for transfers between devices: none -> 49 us  [_render_desk(): lax.ppermute(base_arr, mesh_dim, [(tick, tick ^ pp) for tick in range(n_n...]
    psum x1, waiting for transfers between devices: 55.5 us -> 6.68 us  [on_device(): lax.psum(part_vir.astype(jnp.float32).astype(jnp.bfloat16), 'col')]
    all_to_all x1 -> x0, waiting for transfers between devices: 46.1 us -> none  [on_device(): lax.all_to_all(spread_planes(occupied_waves), 'row', split_axis=1, concat...]
    all_to_all x1, waiting for transfers between devices: 23 us -> 0.01 us  [on_device(): lax.all_to_all(pick_rows(occupied_waves), 'row', split_axis=1, concat_axi...]
    ppermute x0 -> x15, starting transfers between devices: none -> 15.8 us  [_render_desk(): lax.ppermute(base_arr, mesh_dim, [(tick, tick ^ pp) for tick in range(n_n...]
    unnamed x28 -> x59, local copies, waits for them, and re-layouts: 55.6 us -> 71.1 us
    another operation x0 -> x2, local copies, waits for them, and re-layouts: none -> 6.73 us
    all_to_all x1 -> x0, starting transfers between devices: 5.24 us -> none  [on_device(): lax.all_to_all(spread_planes(occupied_waves), 'row', split_axis=1, concat...]
  transfers between devices with their start and end apart: 9 -> 23, of which waited for: 7 -> 15; matrix products, arithmetic and copies ran while one was open for 26% -> 32% of each run, Pallas kernels for 0% -> 0%
where the time goes in v1:
time: 468 us; the launch traced here: 460 us
  local copies, waits for them, and re-layouts  196 us (42%)
  waiting for transfers between devices  95.3 us (20%)
  matrix products  67.9 us (15%)
  starting transfers between devices  55.3 us (12%)
  other arithmetic  30.8 us (7%)
  between operations  15 us (3%)
    unnamed x59, local copies, waits for them, and re-layouts  71.1 us
    dot_general x10, matrix products, apply_table(): return jnp.einsum(form, data, table, precision=lax.Precision.HIGHEST)  64.6 us
    ppermute x15, waiting for transfers between devices, _render_desk(): lax.ppermute(base_arr, mesh_dim, [(tick, tick ^ pp) for tick in range(n_n...  49 us
    ppermute x15, starting transfers between devices, _render_desk(): lax.ppermute(base_arr, mesh_dim, [(tick, tick ^ pp) for tick in range(n_n...  15.8 us
    reshape x2, local copies, waits for them, and re-layouts, on_device(): imag_part.reshape(blocked)  15.5 us
    reshape x2, local copies, waits for them, and re-layouts, on_device(): real_part.reshape(blocked)  15.5 us
    all_to_all x2, local copies, waits for them, and re-layouts, on_device(): lax.all_to_all(real_part.reshape(blocked), 'row', split_axis=3, concat_ax...  14.7 us
    all_to_all x1, waiting for transfers between devices, on_device(): lax.all_to_all(imag_part.reshape(blocked), 'row', split_axis=3, concat_ax...  14.2 us
  transfers between devices with their start and end apart: 23, of which 15 were waited for; matrix products, arithmetic and copies ran while one was open for 32% of the time, Pallas kernels for 0%

profile of v1, /device:TPU:10, one launch (start us, length us, event | category | flops | bytes accessed | tf_op | source)
XLA Modules:
  0.0 460.1 jit_solution(5676458131485392163)
XLA Ops:
  9.4 6.2 %all-to-all-start.1 = ((bf16[32,16,512]{2,0,1:T(8,128)(2,1)}), bf16[32,16,512]{2,0,1:T(8,128)(2,1)S(1)}, u32[]{:S(2)}, u32[]{:S(2)}) async-start(bf16[32,16,512]{2,0,1:T(8,128)(2,1)} %broadcast_in_dim.11), calls=%async_computation.1 | async-start | bytes 1048576 | tf_op jit(solution)/shard_map/all_to_all | solution.py:109
  20.4 8.6 %all-to-all-done.1 = bf16[32,16,512]{2,0,1:T(8,128)(2,1)S(1)} async-done(((bf16[32,16,512]{2,0,1:T(8,128)(2,1)}), bf16[32,16,512]{2,0,1:T(8,128)(2,1)S(1)}, u32[]{:S(2)}, u32[]{:S(2)}) %all-to-all-start.1) | async-done | bytes 524320 | tf_op jit(solution)/shard_map/all_to_all | solution.py:109
  30.1 5.2 %all-to-all-start = ((bf16[64,16,512]{2,0,1:T(8,128)(2,1)}), bf16[64,16,512]{2,0,1:T(8,128)(2,1)S(1)}, u32[]{:S(2)}, u32[]{:S(2)}) async-start(bf16[64,16,512]{2,0,1:T(8,128)(2,1)} %broadcast_in_dim.9), calls=%async_computation | async-start | bytes 2097152 | tf_op jit(solution)/shard_map/all_to_all | solution.py:108
  35.3 6.1 %constant_dynamic-slice_fusion = (bf16[64,1,1024]{2,1,0:T(2,128)(2,1)S(1)}, bf16[64,1,1024]{2,1,0:T(2,128)(2,1)S(1)}, bf16[64,1,1024]{2,1,0:T(2,128)(2,1)S(1)}, ...) fusion(bf16[64,16,1024]{2,1,0:T(8,128)(2,1)S(1)} %bitcast.196, ...), kind=kLoop, calls=%fused_computation.88 | loop fusion | bytes 4194368 | tf_op jit(solution)/shard_map/dynamic-slice.15
  62.2 6.3 %collective-permute-done.5 = bf16[64,1024]{1,0:T(8,128)(2,1)S(1)} collective-permute-done((bf16[64,1024]{1,0:T(8,128)(2,1)S(1)}, bf16[64,1024]{1,0:T(8,128)(2,1)S(1)}, u32[]{:S(2)}, u32[]{:S(2)}) %collective-permute-start.5) | collective-permute-done | bytes 131104 | tf_op jit(solution)/shard_map/ppermute | solution.py:35
  71.0 6.3 %all-to-all-start.2 = ((bf16[32,16,1024]{2,0,1:T(8,128)(2,1)}), bf16[32,16,1024]{2,0,1:T(8,128)(2,1)S(1)}, u32[]{:S(2)}, u32[]{:S(2)}) async-start(bf16[32,16,1024]{2,0,1:T(8,128)(2,1)} %bitcast.166), calls=%async_computation.2 | async-start | bytes 2097152 | tf_op jit(solution)/shard_map/all_to_all | solution.py:103
  88.8 31.4 %collective-permute-done.11 = bf16[64,1024]{1,0:T(8,128)(2,1)S(1)} collective-permute-done((bf16[64,1024]{1,0:T(8,128)(2,1)S(1)}, bf16[64,1024]{1,0:T(8,128)(2,1)S(1)}, u32[]{:S(2)}, u32[]{:S(2)}) %collective-permute-start.11) | collective-permute-done | bytes 131104 | tf_op jit(solution)/shard_map/ppermute | solution.py:35
  122.4 3.3 collective-permute-done.13
  130.4 6.7 %all-reduce.3.cloned.1.call-done = (bf16[512,512]{1,0:T(8,128)(2,1)}, bf16[1024,512]{1,0:T(8,128)(2,1)}) async-done(((bf16[512,512]{1,0:T(8,128)(2,1)}, bf16[1024,512]{1,0:T(8,128)(2,1)}), (bf16[512,512]{1,0:T(8,128)(2,1)}, bf16[1024,512]{1,0:T(8,128)(2,1)})) %all-reduce.3.cloned.1.call-update) | async-done | bytes 1572880 | tf_op jit(solution)/shard_map/psum | solution.py:113
  144.4 3.0 fusion.1
  147.4 4.8 %subtract_bitcast_fusion = f32[32,1,32,512]{3,2,0,1:T(8,128)} fusion(f32[32,32,512]{2,0,1:T(8,128)S(1)} %fusion.1, f32[32,32,512]{2,0,1:T(8,128)S(1)} %fusion.30), kind=kOutput, calls=%fused_computation.5 | convolution fusion | flops 201865216 | bytes 6291456 | tf_op jit(solution)/shard_map/wabr,bv->wavr/dot_general | solution.py:50
  152.2 6.2 %reshape.134 = f32[32,1,32,16,32]{4,3,2,0,1:T(8,128)} reshape(f32[32,1,32,512]{3,2,0,1:T(8,128)} %subtract_bitcast_fusion) | data formatting | bytes 4194304 | tf_op jit(solution)/shard_map/reshape | solution.py:136
  158.4 9.3 %copy.114 = f32[32,1,32,16,32]{4,2,0,1,3:T(8,128)} copy(f32[32,1,32,16,32]{4,3,2,0,1:T(8,128)} %reshape.134) | data formatting | bytes 4194304 | tf_op jit(solution)/shard_map/reshape | solution.py:136
  167.7 8.6 %reshape.155 = f32[16,1,32768]{2,1,0:T(1,128)} reshape(f32[16,1,32,32,32]{4,3,2,1,0:T(8,128)} %bitcast.190) | data formatting | bytes 4194304
  176.3 6.1 %all-to-all-start.5 = ((f32[16,1,32768]{2,1,0:T(1,128)}), f32[16,1,32768]{2,1,0:T(1,128)}, u32[]{:S(2)}, u32[]{:S(2)}) async-start(f32[16,1,32768]{2,1,0:T(1,128)} %reshape.155), calls=%async_computation.5 | async-start | bytes 4194304 | tf_op jit(solution)/shard_map/all_to_all | solution.py:135
  182.4 4.6 fusion.3
  186.9 4.4 add_bitcast_fusion
  191.3 6.2 %reshape.131 = f32[32,1,32,16,32]{4,3,2,0,1:T(8,128)} reshape(f32[32,1,32,512]{3,2,0,1:T(8,128)} %add_bitcast_fusion) | data formatting | bytes 4194304 | tf_op jit(solution)/shard_map/reshape | solution.py:127
  197.5 9.3 %copy.115 = f32[32,1,32,16,32]{4,2,0,1,3:T(8,128)} copy(f32[32,1,32,16,32]{4,3,2,0,1:T(8,128)} %reshape.131) | data formatting | bytes 4194304 | tf_op jit(solution)/shard_map/reshape | solution.py:127
  206.8 8.6 %reshape.151 = f32[16,1,32768]{2,1,0:T(1,128)} reshape(f32[16,1,32,32,32]{4,3,2,1,0:T(8,128)} %bitcast.191) | data formatting | bytes 4194304
  215.4 14.2 %all-to-all-done.5 = f32[16,1,32768]{2,1,0:T(1,128)} async-done(((f32[16,1,32768]{2,1,0:T(1,128)}), f32[16,1,32768]{2,1,0:T(1,128)}, u32[]{:S(2)}, u32[]{:S(2)}) %all-to-all-start.5) | async-done | bytes 2097184 | tf_op jit(solution)/shard_map/all_to_all | solution.py:135
  229.6 5.4 %all-to-all-start.3 = ((f32[16,1,32768]{2,1,0:T(1,128)}), f32[16,1,32768]{2,1,0:T(1,128)}, u32[]{:S(2)}, u32[]{:S(2)}) async-start(f32[16,1,32768]{2,1,0:T(1,128)} %reshape.151), calls=%async_computation.3 | async-start | bytes 4194304 | tf_op jit(solution)/shard_map/all_to_all | solution.py:126
  235.5 7.2 %reduce.2 = f32[16,32768]{1,0:T(8,128)S(1)} reduce(f32[16,1,32768]{2,1,0:T(1,128)} %all-to-all-done.5, f32[]{:T(128)} %broadcast.135), dimensions={1}, to_apply=%all_to_all.80.reduce_sub_computation | reduce | bytes 4194308 | tf_op jit(solution)/shard_map/all_to_all | solution.py:135
  242.7 5.0 %reshape.156 = f32[16,1,32,32,32]{4,3,2,1,0:T(8,128)} reshape(f32[16,32768]{1,0:T(8,128)S(1)} %reduce.2) | data formatting | bytes 4194304
  247.7 14.2 %copy.42 = f32[32,1,32,16,32]{4,3,2,1,0:T(8,128)} copy(f32[32,1,32,16,32]{4,2,0,1,3:T(8,128)} %bitcast.192) | data formatting | bytes 4194304 | tf_op jit(solution)/shard_map/all_to_all | solution.py:135
  261.9 6.8 %reshape.157 = f32[2,1,262144]{2,1,0:T(1,128)} reshape(f32[32,1,32,16,32]{4,3,2,1,0:T(8,128)} %copy.42) | data formatting | bytes 4194304
  268.7 13.4 %all-to-all-done.3 = f32[16,1,32768]{2,1,0:T(1,128)} async-done(((f32[16,1,32768]{2,1,0:T(1,128)}), f32[16,1,32768]{2,1,0:T(1,128)}, u32[]{:S(2)}, u32[]{:S(2)}) %all-to-all-start.3) | async-done | bytes 2097184 | tf_op jit(solution)/shard_map/all_to_all | solution.py:126
  282.1 5.2 %all-to-all-start.6 = ((f32[2,1,262144]{2,1,0:T(1,128)}), f32[2,1,262144]{2,1,0:T(1,128)}, u32[]{:S(2)}, u32[]{:S(2)}) async-start(f32[2,1,262144]{2,1,0:T(1,128)} %reshape.157), calls=%async_computation.6 | async-start | bytes 4194304 | tf_op jit(solution)/shard_map/all_to_all | solution.py:134
  287.3 7.2 %reduce = f32[16,32768]{1,0:T(8,128)S(1)} reduce(f32[16,1,32768]{2,1,0:T(1,128)} %all-to-all-done.3, f32[]{:T(128)} %broadcast.135), dimensions={1}, to_apply=%all_to_all.76.reduce_sub_computation | reduce | bytes 4194308 | tf_op jit(solution)/shard_map/all_to_all | solution.py:126
  294.5 4.8 %reshape.152 = f32[16,1,32,32,32]{4,3,2,1,0:T(8,128)} reshape(f32[16,32768]{1,0:T(8,128)S(1)} %reduce) | data formatting | bytes 4194304
  299.3 14.2 %copy.37 = f32[32,1,32,16,32]{4,3,2,1,0:T(8,128)} copy(f32[32,1,32,16,32]{4,2,0,1,3:T(8,128)} %bitcast.193) | data formatting | bytes 4194304 | tf_op jit(solution)/shard_map/all_to_all | solution.py:126
  313.5 6.8 %reshape.153 = f32[2,1,262144]{2,1,0:T(1,128)} reshape(f32[32,1,32,16,32]{4,3,2,1,0:T(8,128)} %copy.37) | data formatting | bytes 4194304
  320.3 4.8 %all-to-all-start.4 = ((f32[2,1,262144]{2,1,0:T(1,128)}), f32[2,1,262144]{2,1,0:T(1,128)}, u32[]{:S(2)}, u32[]{:S(2)}) async-start(f32[2,1,262144]{2,1,0:T(1,128)} %reshape.153), calls=%async_computation.4 | async-start | bytes 4194304 | tf_op jit(solution)/shard_map/all_to_all | solution.py:125
  325.2 8.2 %reduce.3 = f32[2,262144]{1,0:T(2,128)S(1)} reduce(f32[2,1,262144]{2,1,0:T(1,128)} %all-to-all-done.6, f32[]{:T(128)} %broadcast.135), dimensions={1}, to_apply=%all_to_all.81.reduce_sub_computation | reduce | bytes 4194308 | tf_op jit(solution)/shard_map/all_to_all | solution.py:134
  333.3 6.4 %reshape.158 = f32[32,1,32,16,32]{4,3,2,1,0:T(8,128)} reshape(f32[2,262144]{1,0:T(2,128)S(1)} %reduce.3) | data formatting | bytes 4194304
  339.8 7.8 %copy.43 = f32[2,16,1,32,16,32]{5,4,0,3,1,2:T(8,128)} copy(f32[2,16,1,32,16,32]{5,4,3,1,0,2:T(8,128)} %bitcast.194) | data formatting | bytes 4194304 | tf_op jit(solution)/shard_map/all_to_all | solution.py:134
  347.5 3.4 all-to-all-done.4
  350.9 8.2 %reduce.1 = f32[2,262144]{1,0:T(2,128)S(1)} reduce(f32[2,1,262144]{2,1,0:T(1,128)} %all-to-all-done.4, f32[]{:T(128)} %broadcast.135), dimensions={1}, to_apply=%all_to_all.77.reduce_sub_computation | reduce | bytes 4194308 | tf_op jit(solution)/shard_map/all_to_all | solution.py:125
  359.1 6.4 %reshape.154 = f32[32,1,32,16,32]{4,3,2,1,0:T(8,128)} reshape(f32[2,262144]{1,0:T(2,128)S(1)} %reduce.1) | data formatting | bytes 4194304
  365.6 4.6 copy.38
  370.2 9.5 %fusion.23 = f32[32,16,32,32]{3,0,2,1:T(8,128)} fusion(f32[16,32,32,32]{3,1,2,0:T(8,128)S(1)} %bitcast.188), kind=kOutput, calls=%fused_computation.63 | convolution fusion | flops 201340928 | bytes 4194304 | tf_op jit(solution)/shard_map/wavr,au->rwuv/dot_general | solution.py:50
  379.7 9.8 %fusion.21 = f32[32,16,32,32]{3,0,2,1:T(8,128)} fusion(f32[16,32,32,32]{3,1,2,0:T(8,128)S(1)} %bitcast.186), kind=kOutput, calls=%fused_computation.61 | convolution fusion | flops 201340928 | bytes 4194304 | tf_op jit(solution)/shard_map/wavr,au->rwuv/dot_general | solution.py:50
  389.5 12.1 %multiply_bitcast_fusion.1 = f32[32,16,32,32]{0,2,3,1:T(8,128)} fusion(f32[32,16,32,32]{3,0,2,1:T(8,128)} %fusion.23, f32[16,32,32,32]{3,1,2,0:T(8,128)S(1)} %bitcast.187), kind=kOutput, calls=%fused_computation.2 | convolution fusion | flops 202389504 | bytes 6291456 | tf_op jit(solution)/shard_map/wavr,au->rwuv/dot_general | solution.py:50
  401.6 12.5 %multiply_bitcast_fusion = f32[32,16,32,32]{0,2,3,1:T(8,128)} fusion(f32[32,16,32,32]{3,0,2,1:T(8,128)} %fusion.21, f32[16,32,32,32]{3,1,2,0:T(8,128)S(1)} %bitcast.189), kind=kOutput, calls=%fused_computation.1 | convolution fusion | flops 202389504 | bytes 6291456 | tf_op jit(solution)/shard_map/wavr,au->rwuv/dot_general | solution.py:50
  414.1 11.6 %copy.45 = f32[32,16,32,32]{3,2,1,0:T(8,128)} copy(f32[32,16,32,32]{0,2,3,1:T(8,128)} %multiply_bitcast_fusion) | data formatting | bytes 4194304 | tf_op jit(solution)/shard_map/mul | solution.py:154
  425.8 7.7 %reshape.138 = f32[32,16,1024]{2,1,0:T(8,128)} reshape(f32[32,16,32,32]{3,2,1,0:T(8,128)} %copy.45) | data formatting | bytes 4194304 | tf_op jit(solution)/shard_map/reshape | solution.py:154
  433.5 11.6 %copy.44 = f32[32,16,32,32]{3,2,1,0:T(8,128)} copy(f32[32,16,32,32]{0,2,3,1:T(8,128)} %multiply_bitcast_fusion.1) | data formatting | bytes 4194304 | tf_op jit(solution)/shard_map/mul | solution.py:154
  445.1 7.7 %reshape.137 = f32[32,16,1024]{2,1,0:T(8,128)} reshape(f32[32,16,32,32]{3,2,1,0:T(8,128)} %copy.44) | data formatting | bytes 4194304 | tf_op jit(solution)/shard_map/reshape | solution.py:154
  (102 shorter events, 57.2 us)
Async XLA Ops:
  9.4 19.5 %all-to-all-start.1 = ((bf16[32,16,512]{2,0,1:T(8,128)(2,1)}), bf16[32,16,512]{2,0,1:T(8,128)(2,1)S(1)}, u32[]{:S(2)}, u32[]{:S(2)}) async-start(bf16[32,16,512]{2,0,1:T(8,128)(2,1)} %broadcast_in_dim.11), calls=%async_computation.1 | async-start | bytes 1048576 | tf_op jit(solution)/shard_map/all_to_all | solution.py:109
  18.5 1.6 copy-start.1
  29.0 1.2 copy-start.4
  30.1 40.9 %all-to-all-start = ((bf16[64,16,512]{2,0,1:T(8,128)(2,1)}), bf16[64,16,512]{2,0,1:T(8,128)(2,1)S(1)}, u32[]{:S(2)}, u32[]{:S(2)}) async-start(bf16[64,16,512]{2,0,1:T(8,128)(2,1)} %broadcast_in_dim.9), calls=%async_computation | async-start | bytes 2097152 | tf_op jit(solution)/shard_map/all_to_all | solution.py:108
  41.4 4.9 %copy-start.2 = (bf16[32,16384]{1,0:T(8,128)(2,1)S(1)}, bf16[32,16384]{1,0:T(8,128)(2,1)}, u32[]{:S(2)}) copy-start(bf16[32,16384]{1,0:T(8,128)(2,1)} %param.5) | copy-start | bytes 3145732
  41.4 6.4 %collective-permute-start = (bf16[64,1024]{1,0:T(8,128)(2,1)S(1)}, bf16[64,1024]{1,0:T(8,128)(2,1)S(1)}, u32[]{:S(2)}, u32[]{:S(2)}) collective-permute-start(bf16[64,1024]{1,0:T(8,128)(2,1)S(1)} %bitcast.219), channel_id=1, source_target_pairs={{0,2},{2,0},{4,6},{6,4},{8,10},{10,8},{12,14},{14,12},{16,18},{18,... | collective-permute-start | bytes 393224 | tf_op jit(solution)/shard_map/ppermute | solution.py:35
  41.6 7.9 %collective-permute-start.1 = (bf16[64,1024]{1,0:T(8,128)(2,1)S(1)}, bf16[64,1024]{1,0:T(8,128)(2,1)S(1)}, u32[]{:S(2)}, u32[]{:S(2)}) collective-permute-start(bf16[64,1024]{1,0:T(8,128)(2,1)S(1)} %bitcast.217), channel_id=1, source_target_pairs={{0,4},{2,6},{4,0},{6,2},{8,12},{10,14},{12,8},{14,10},{16,20},{18,... | collective-permute-start | bytes 393224 | tf_op jit(solution)/shard_map/ppermute | solution.py:35
  42.3 11.6 %collective-permute-start.2 = (bf16[64,1024]{1,0:T(8,128)(2,1)S(1)}, bf16[64,1024]{1,0:T(8,128)(2,1)S(1)}, u32[]{:S(2)}, u32[]{:S(2)}) collective-permute-start(bf16[64,1024]{1,0:T(8,128)(2,1)S(1)} %bitcast.216), channel_id=1, source_target_pairs={{0,6},{2,4},{4,2},{6,0},{8,14},{10,12},{12,10},{14,8},{16,22},{18,... | collective-permute-start | bytes 393224 | tf_op jit(solution)/shard_map/ppermute | solution.py:35
  43.6 13.7 %collective-permute-start.3 = (bf16[64,1024]{1,0:T(8,128)(2,1)S(1)}, bf16[64,1024]{1,0:T(8,128)(2,1)S(1)}, u32[]{:S(2)}, u32[]{:S(2)}) collective-permute-start(bf16[64,1024]{1,0:T(8,128)(2,1)S(1)} %bitcast.215), channel_id=1, source_target_pairs={{0,8},{2,10},{4,12},{6,14},{8,0},{10,2},{12,4},{14,6},{16,24},{18,... | collective-permute-start | bytes 393224 | tf_op jit(solution)/shard_map/ppermute | solution.py:35
  44.3 14.8 %collective-permute-start.4 = (bf16[64,1024]{1,0:T(8,128)(2,1)S(1)}, bf16[64,1024]{1,0:T(8,128)(2,1)S(1)}, u32[]{:S(2)}, u32[]{:S(2)}) collective-permute-start(bf16[64,1024]{1,0:T(8,128)(2,1)S(1)} %bitcast.214), channel_id=1, source_target_pairs={{0,10},{2,8},{4,14},{6,12},{8,2},{10,0},{12,6},{14,4},{16,26},{18,... | collective-permute-start | bytes 393224 | tf_op jit(solution)/shard_map/ppermute | solution.py:35
  47.8 20.7 %collective-permute-start.5 = (bf16[64,1024]{1,0:T(8,128)(2,1)S(1)}, bf16[64,1024]{1,0:T(8,128)(2,1)S(1)}, u32[]{:S(2)}, u32[]{:S(2)}) collective-permute-start(bf16[64,1024]{1,0:T(8,128)(2,1)S(1)} %bitcast.218), channel_id=1, source_target_pairs={{0,12},{2,14},{4,8},{6,10},{8,4},{10,6},{12,0},{14,2},{16,28},{18,... | collective-permute-start | bytes 393224 | tf_op jit(solution)/shard_map/ppermute | solution.py:35
  49.6 28.1 %collective-permute-start.6 = (bf16[64,1024]{1,0:T(8,128)(2,1)S(1)}, bf16[64,1024]{1,0:T(8,128)(2,1)}, u32[]{:S(2)}, u32[]{:S(2)}) collective-permute-start(bf16[64,1024]{1,0:T(8,128)(2,1)S(1)} %bitcast.213), channel_id=1, source_target_pairs={{0,14},{2,12},{4,10},{6,8},{8,6},{10,4},{12,2},{14,0},{16,30},{18,... | collective-permute-start | bytes 393224 | tf_op jit(solution)/shard_map/ppermute | solution.py:35
  53.9 26.9 %collective-permute-start.7 = (bf16[64,1024]{1,0:T(8,128)(2,1)S(1)}, bf16[64,1024]{1,0:T(8,128)(2,1)}, u32[]{:S(2)}, u32[]{:S(2)}) collective-permute-start(bf16[64,1024]{1,0:T(8,128)(2,1)S(1)} %bitcast.212), channel_id=1, source_target_pairs={{0,16},{2,18},{4,20},{6,22},{8,24},{10,26},{12,28},{14,30},{16,0},... | collective-permute-start | bytes 393224 | tf_op jit(solution)/shard_map/ppermute | solution.py:35
  57.3 25.0 %collective-permute-start.8 = (bf16[64,1024]{1,0:T(8,128)(2,1)S(1)}, bf16[64,1024]{1,0:T(8,128)(2,1)S(1)}, u32[]{:S(2)}, u32[]{:S(2)}) collective-permute-start(bf16[64,1024]{1,0:T(8,128)(2,1)S(1)} %bitcast.211), channel_id=1, source_target_pairs={{0,18},{2,16},{4,22},{6,20},{8,26},{10,24},{12,30},{14,28},{16,2},... | collective-permute-start | bytes 393224 | tf_op jit(solution)/shard_map/ppermute | solution.py:35
  59.1 25.5 %collective-permute-start.9 = (bf16[64,1024]{1,0:T(8,128)(2,1)S(1)}, bf16[64,1024]{1,0:T(8,128)(2,1)S(1)}, u32[]{:S(2)}, u32[]{:S(2)}) collective-permute-start(bf16[64,1024]{1,0:T(8,128)(2,1)S(1)} %bitcast.210), channel_id=1, source_target_pairs={{0,20},{2,22},{4,16},{6,18},{8,28},{10,30},{12,24},{14,26},{16,4},... | collective-permute-start | bytes 393224 | tf_op jit(solution)/shard_map/ppermute | solution.py:35
  68.5 18.7 %collective-permute-start.10 = (bf16[64,1024]{1,0:T(8,128)(2,1)S(1)}, bf16[64,1024]{1,0:T(8,128)(2,1)}, u32[]{:S(2)}, u32[]{:S(2)}) collective-permute-start(bf16[64,1024]{1,0:T(8,128)(2,1)S(1)} %bitcast.209), channel_id=1, source_target_pairs={{0,22},{2,20},{4,18},{6,16},{8,30},{10,28},{12,26},{14,24},{16,6},... | collective-permute-start | bytes 393224 | tf_op jit(solution)/shard_map/ppermute | solution.py:35
  71.0 11.3 %copy-start.3 = (bf16[64,16,512]{2,0,1:T(8,128)(2,1)}, bf16[64,16,512]{2,0,1:T(8,128)(2,1)S(1)}, u32[]{:S(2)}) copy-start(bf16[64,16,512]{2,0,1:T(8,128)(2,1)S(1)} %all-to-all-done) | copy-start | bytes 3145732
  71.0 59.4 %all-to-all-start.2 = ((bf16[32,16,1024]{2,0,1:T(8,128)(2,1)}), bf16[32,16,1024]{2,0,1:T(8,128)(2,1)S(1)}, u32[]{:S(2)}, u32[]{:S(2)}) async-start(bf16[32,16,1024]{2,0,1:T(8,128)(2,1)} %bitcast.166), calls=%async_computation.2 | async-start | bytes 2097152 | tf_op jit(solution)/shard_map/all_to_all | solution.py:103
  77.4 59.7 %all-reduce.3.cloned.1.call-start = ((), (), s32[]{:S(2)}) async-start(), calls=%async_computation.7 | async-start | bytes 3145728 | tf_op jit(solution)/shard_map/psum | solution.py:113
  77.7 42.6 %collective-permute-start.11 = (bf16[64,1024]{1,0:T(8,128)(2,1)S(1)}, bf16[64,1024]{1,0:T(8,128)(2,1)S(1)}, u32[]{:S(2)}, u32[]{:S(2)}) collective-permute-start(bf16[64,1024]{1,0:T(8,128)(2,1)S(1)} %bitcast.208), channel_id=1, source_target_pairs={{0,24},{2,26},{4,28},{6,30},{8,16},{10,18},{12,20},{14,22},{16,8},... | collective-permute-start | bytes 393224 | tf_op jit(solution)/shard_map/ppermute | solution.py:35
  80.8 41.0 %collective-permute-start.12 = (bf16[64,1024]{1,0:T(8,128)(2,1)S(1)}, bf16[64,1024]{1,0:T(8,128)(2,1)S(1)}, u32[]{:S(2)}, u32[]{:S(2)}) collective-permute-start(bf16[64,1024]{1,0:T(8,128)(2,1)S(1)} %bitcast.207), channel_id=1, source_target_pairs={{0,26},{2,24},{4,30},{6,28},{8,18},{10,16},{12,22},{14,20},{16,10}... | collective-permute-start | bytes 393224 | tf_op jit(solution)/shard_map/ppermute | solution.py:35
  82.4 43.4 %collective-permute-start.13 = (bf16[64,1024]{1,0:T(8,128)(2,1)S(1)}, bf16[64,1024]{1,0:T(8,128)(2,1)S(1)}, u32[]{:S(2)}, u32[]{:S(2)}) collective-permute-start(bf16[64,1024]{1,0:T(8,128)(2,1)S(1)} %bitcast.206), channel_id=1, source_target_pairs={{0,28},{2,30},{4,24},{6,26},{8,20},{10,22},{12,16},{14,18},{16,12}... | collective-permute-start | bytes 393224 | tf_op jit(solution)/shard_map/ppermute | solution.py:35
  84.6 42.9 %collective-permute-start.14 = (bf16[64,1024]{1,0:T(8,128)(2,1)S(1)}, bf16[64,1024]{1,0:T(8,128)(2,1)S(1)}, u32[]{:S(2)}, u32[]{:S(2)}) collective-permute-start(bf16[64,1024]{1,0:T(8,128)(2,1)S(1)} %bitcast.205), channel_id=1, source_target_pairs={{0,30},{2,28},{4,26},{6,24},{8,22},{10,20},{12,18},{14,16},{16,14}... | collective-permute-start | bytes 393224 | tf_op jit(solution)/shard_map/ppermute | solution.py:35
  128.1 9.0 %copy-start.5 = (f32[512]{0:T(512)S(1)}, f32[512]{0:T(512)}, u32[]{:S(2)}) copy-start(f32[512]{0:T(512)} %param.7) | copy-start | bytes 6148
  130.4 8.7 %copy-start.7 = (f32[1024]{0:T(1024)S(1)}, f32[1024]{0:T(1024)}, u32[]{:S(2)}) copy-start(f32[1024]{0:T(1024)} %param.6) | copy-start | bytes 12292
  137.1 2.0 copy-start.6
  142.4 2.0 copy-start
  176.3 53.3 %all-to-all-start.5 = ((f32[16,1,32768]{2,1,0:T(1,128)}), f32[16,1,32768]{2,1,0:T(1,128)}, u32[]{:S(2)}, u32[]{:S(2)}) async-start(f32[16,1,32768]{2,1,0:T(1,128)} %reshape.155), calls=%async_computation.5 | async-start | bytes 4194304 | tf_op jit(solution)/shard_map/all_to_all | solution.py:135
  229.6 52.5 %all-to-all-start.3 = ((f32[16,1,32768]{2,1,0:T(1,128)}), f32[16,1,32768]{2,1,0:T(1,128)}, u32[]{:S(2)}, u32[]{:S(2)}) async-start(f32[16,1,32768]{2,1,0:T(1,128)} %reshape.151), calls=%async_computation.3 | async-start | bytes 4194304 | tf_op jit(solution)/shard_map/all_to_all | solution.py:126
  282.1 38.3 %all-to-all-start.6 = ((f32[2,1,262144]{2,1,0:T(1,128)}), f32[2,1,262144]{2,1,0:T(1,128)}, u32[]{:S(2)}, u32[]{:S(2)}) async-start(f32[2,1,262144]{2,1,0:T(1,128)} %reshape.157), calls=%async_computation.6 | async-start | bytes 4194304 | tf_op jit(solution)/shard_map/all_to_all | solution.py:134
  320.3 30.6 %all-to-all-start.4 = ((f32[2,1,262144]{2,1,0:T(1,128)}), f32[2,1,262144]{2,1,0:T(1,128)}, u32[]{:S(2)}, u32[]{:S(2)}) async-start(f32[2,1,262144]{2,1,0:T(1,128)} %reshape.153), calls=%async_computation.4 | async-start | bytes 4194304 | tf_op jit(solution)/shard_map/all_to_all | solution.py:125
  365.6 14.1 %slice-start = ((s8[8388608]{0:T(1024)(128)(4,1)}), s8[4194304]{0:T(1024)(128)(4,1)S(1)}, s32[]{:S(2)}) async-start(s8[8388608]{0:T(1024)(128)(4,1)} %bitcast.184), calls=%async_computation.8 | async-start | bytes 8388608
  370.1 9.5 %slice-start.1 = ((s8[8388608]{0:T(1024)(128)(4,1)}), s8[4194304]{0:T(1024)(128)(4,1)S(1)}, s32[]{:S(2)}) async-start(s8[8388608]{0:T(1024)(128)(4,1)} %bitcast.184), calls=%async_computation.9 | async-start | bytes 8388608
Sparse Core Ops, SparseCore 0:
  82.5 54.5 all-reduce.2
